TPU v7x, 32 devices: a whole 2x2x4 slice. The times are simulated.
32 devices in a mesh: tm: 8 (over y, x, core), space: 4 (over z).
Axes of the slice: x: 2, y: 2, z: 4, core: 2. Of those that a mesh axis runs over, the one named last changes fastest.
Arguments:
- rhs: float32 [16, 1024, 1024], P('tm', 'space'), may hold values from -6 to 6
- guess: float32 [16, 1024, 1024], P('tm', 'space'), may hold values from -6 to 6
- diffusion: float32 [1024, 1024], P('space'), may hold values from 0.2 to 2
Outputs:
- solution: float32 [16, 1024, 1024], P('tm', 'space')
- norms: float32 [6], replicated
All inputs are finite; a program needn't handle non-finite values.
Results may differ from a plain program's by a relative error of at most 0.0001.
Values sent between devices are 32-bit elements; how exact they have to be, the bound alone decides.
A program may use at most 64 MiB of HBM per device.

v0:
```python
import jax
import jax.numpy as jnp
from jax import lax
from jax.sharding import PartitionSpec as P

LEVELS = 5
damping = 0.8


def with_halo(block, sides, width):
    for axis, dim in sides:
        count = lax.axis_size(axis)
        forward = [(i, i + 1) for i in range(count - 1)]
        backward = [(target, source) for source, target in forward]
        low = lax.ppermute(
            lax.slice_in_dim(block, block.shape[dim] - width, None, axis=dim), axis, forward
        )
        high = lax.ppermute(lax.slice_in_dim(block, 0, width, axis=dim), axis, backward)
        block = jnp.concatenate([low, block, high], axis=dim)
    return block


def shifted(value, axis, steps):
    count = lax.axis_size(axis)
    first, last = (max(0, -steps), min(count, count - steps))
    return lax.ppermute(value, axis, [(source, source + steps) for source in range(first, last)])


def from_partner(value, axis, apart):
    mask = 2**apart
    pairs = [(source, source ^ mask) for source in range(lax.axis_size(axis))]
    return lax.ppermute(value, axis, pairs)


def neighbours(field):
    rows = with_halo(field, (("space", 1),), 1)
    padded = jnp.pad(rows, ((0, 0), (0, 0), (1, 1)))
    total = padded[:, 2:, 1:-1] + padded[:, :-2, 1:-1]
    total = total + padded[:, 1:-1, 2:] + padded[:, 1:-1, :-2]
    return total


def residual(field, source, scaled, diag, stride):
    earlier = shifted(field[-1:], "tm", stride)
    before = jnp.concatenate([earlier, field[:-1]], axis=0)
    image = diag * field - scaled * neighbours(field) - before
    return source - image


def stride_of(level):
    if level == 0:
        return 1
    return 2 ** (level - 1)


def body(rhs, guess, diffusion):
    position = lax.axis_index("tm")
    cells = rhs.shape[1] * lax.axis_size("space") * rhs.shape[2]
    partials = []

    def weight_of(level):
        if level <= 1:
            return jnp.float32(1.0)
        stride = stride_of(level)
        return jnp.where(position % stride == stride - 1, 1.0, 0.0).astype(jnp.float32)

    def record(resid, level):
        local_part = jnp.sum(resid * resid) * weight_of(level)
        partials.append(local_part)

    sources = [rhs]
    fields = []
    field = guess
    for level in range(LEVELS - 1):
        source = sources[level]
        scaled = 2.0**level * diffusion
        diag = 1.0 + 4.0 * scaled
        stride = stride_of(level)
        if level == 0:
            field = field + damping * residual(field, source, scaled, diag, stride) / diag
        else:
            field = damping * source / diag
        resid = residual(field, source, scaled, diag, stride)
        record(resid, level)
        fields.append(field)
        if level == 0:
            coarse = resid[0:1] + resid[1:2]
        else:
            coarse = resid + from_partner(resid, "tm", level - 1)
        sources.append(coarse)
    level = LEVELS - 1
    source = sources[level]
    scaled = 2.0**level * diffusion
    diag = 1.0 + 4.0 * scaled
    stride = stride_of(level)
    field = damping * source / diag
    field = field + damping * residual(field, source, scaled, diag, stride) / diag
    resid = residual(field, source, scaled, diag, stride)
    record(resid, level)
    correction = field
    for level in range(LEVELS - 2, -1, -1):
        scaled = 2.0**level * diffusion
        diag = 1.0 + 4.0 * scaled
        stride = stride_of(level)
        field = fields[level] + correction
        field = field + damping * residual(field, sources[level], scaled, diag, stride) / diag
        correction = field
    scaled = 1.0 * diffusion
    diag = 1.0 + 4.0 * scaled
    resid = residual(correction, rhs, scaled, diag, 1)
    record(resid, 0)
    totals = lax.psum(jnp.stack(partials), ("tm", "space"))
    norms = jnp.sqrt(totals / cells)
    return (correction, norms)


def solution(mesh):
    in_specs = (P("tm", "space", None), P("tm", "space", None), P("space", None))
    out_specs = (P("tm", "space", None), P())
    return jax.shard_map(body, mesh=mesh, in_specs=in_specs, out_specs=out_specs, check_vma=False)
```

profile of v0, /device:TPU:0, one launch (start us, length us, event | category | flops | bytes accessed | tf_op | source)
XLA Modules:
  0.0 330.1 jit_solution(2631628433382767291)
XLA Ops:
  6.3 4.9 %collective-permute-start.1 = (f32[2,1,1024]{2,1,0:T(1,128)S(1)}, f32[2,1,1024]{2,1,0:T(1,128)S(1)}, u32[]{:S(2)}, u32[]{:S(2)}) collective-permute-start(f32[2,1,1024]{2,1,0:T(1,128)S(1)} %get-tuple-element.32), channel_id=1, source_target_pairs={{0,1},{1,2},{2,3},{4,5},{5,6},{6,7},{8,9},{9,10},{10,11},{12,13},{... | collective-permute-start | bytes 24584 | tf_op jit(solution)/shard_map/ppermute | solution.py:15
  15.5 7.8 %collective-permute-start.5 = (f32[1,256,1024]{2,1,0:T(8,128)S(1)}, f32[1,256,1024]{2,1,0:T(8,128)S(1)}, u32[]{:S(2)}, u32[]{:S(2)}) collective-permute-start(f32[1,256,1024]{2,1,0:T(8,128)S(1)} %get-tuple-element.28), channel_id=1, source_target_pairs={{0,4},{4,8},{8,12},{12,16},{16,20},{20,24},{24,28},{1,5},{5,9},{9,... | collective-permute-start | bytes 3145736 | tf_op jit(solution)/shard_map/ppermute | solution.py:26
  24.6 4.5 %collective-permute-start.4 = (f32[2,1,1024]{2,1,0:T(1,128)S(1)}, f32[2,1,1024]{2,1,0:T(1,128)S(1)}, u32[]{:S(2)}, u32[]{:S(2)}) collective-permute-start(f32[2,1,1024]{2,1,0:T(1,128)S(1)} %get-tuple-element.26), channel_id=1, source_target_pairs={{0,1},{1,2},{2,3},{4,5},{5,6},{6,7},{8,9},{9,10},{10,11},{12,13},{... | collective-permute-start | bytes 24584 | tf_op jit(solution)/shard_map/ppermute | solution.py:15
  34.0 8.1 %collective-permute-start.8 = (f32[1,256,1024]{2,1,0:T(8,128)S(1)}, f32[1,256,1024]{2,1,0:T(8,128)S(1)}, u32[]{:S(2)}, u32[]{:S(2)}) collective-permute-start(f32[1,256,1024]{2,1,0:T(8,128)S(1)} %bitcast_divide_fusion.3), channel_id=1, source_target_pairs={{0,4},{4,8},{8,12},{12,16},{16,20},{20,24},{24,28},{1,5},{5,9},{9,... | collective-permute-start | bytes 3145736 | tf_op jit(solution)/shard_map/ppermute | solution.py:26
  43.4 4.5 %collective-permute-start.7 = (f32[1,1,1024]{2,1,0:T(1,128)S(1)}, f32[1,1,1024]{2,1,0:T(1,128)S(1)}, u32[]{:S(2)}, u32[]{:S(2)}) collective-permute-start(f32[1,1,1024]{2,1,0:T(1,128)S(1)} %get-tuple-element.48), channel_id=1, source_target_pairs={{0,1},{1,2},{2,3},{4,5},{5,6},{6,7},{8,9},{9,10},{10,11},{12,13},{... | collective-permute-start | bytes 12296 | tf_op jit(solution)/shard_map/ppermute | solution.py:15
  51.2 6.5 %collective-permute-start.9 = (f32[1,256,1024]{2,1,0:T(8,128)S(1)}, f32[1,256,1024]{2,1,0:T(8,128)S(1)}, u32[]{:S(2)}, u32[]{:S(2)}) collective-permute-start(f32[1,256,1024]{2,1,0:T(8,128)S(1)} %get-tuple-element.7), channel_id=1, source_target_pairs={{0,4},{4,0},{8,12},{12,8},{16,20},{20,16},{24,28},{28,24},{1,5},{5... | collective-permute-start | bytes 3145736 | tf_op jit(solution)/shard_map/ppermute | solution.py:32
  60.4 5.3 %collective-permute-start.12 = (f32[1,256,1024]{2,1,0:T(8,128)S(1)}, f32[1,256,1024]{2,1,0:T(8,128)S(1)}, u32[]{:S(2)}, u32[]{:S(2)}) collective-permute-start(f32[1,256,1024]{2,1,0:T(8,128)S(1)} %get-tuple-element.16), channel_id=1, source_target_pairs={{0,8},{4,12},{8,16},{12,20},{16,24},{20,28},{1,9},{5,13},{9,17},{1... | collective-permute-start | bytes 3145736 | tf_op jit(solution)/shard_map/ppermute | solution.py:26
  67.0 4.5 %collective-permute-start.11 = (f32[1,1,1024]{2,1,0:T(1,128)S(1)}, f32[1,1,1024]{2,1,0:T(1,128)S(1)}, u32[]{:S(2)}, u32[]{:S(2)}) collective-permute-start(f32[1,1,1024]{2,1,0:T(1,128)S(1)} %get-tuple-element.46), channel_id=1, source_target_pairs={{0,1},{1,2},{2,3},{4,5},{5,6},{6,7},{8,9},{9,10},{10,11},{12,13},{... | collective-permute-start | bytes 12296 | tf_op jit(solution)/shard_map/ppermute | solution.py:15
  73.2 15.3 %collective-permute-done.12 = f32[1,256,1024]{2,1,0:T(8,128)S(1)} collective-permute-done((f32[1,256,1024]{2,1,0:T(8,128)S(1)}, f32[1,256,1024]{2,1,0:T(8,128)S(1)}, u32[]{:S(2)}, u32[]{:S(2)}) %collective-permute-start.12) | collective-permute-done | bytes 1048608 | tf_op jit(solution)/shard_map/ppermute | solution.py:26
  90.0 3.4 %collective-permute-start.13 = (f32[1,256,1024]{2,1,0:T(8,128)S(1)}, f32[1,256,1024]{2,1,0:T(8,128)S(1)}, u32[]{:S(2)}, u32[]{:S(2)}) collective-permute-start(f32[1,256,1024]{2,1,0:T(8,128)S(1)} %get-tuple-element.5), channel_id=1, source_target_pairs={{0,8},{4,12},{8,0},{12,4},{16,24},{20,28},{24,16},{28,20},{1,9},{5... | collective-permute-start | bytes 3145736 | tf_op jit(solution)/shard_map/ppermute | solution.py:32
  93.4 22.6 %collective-permute-done.13 = f32[1,256,1024]{2,1,0:T(8,128)S(1)} collective-permute-done((f32[1,256,1024]{2,1,0:T(8,128)S(1)}, f32[1,256,1024]{2,1,0:T(8,128)S(1)}, u32[]{:S(2)}, u32[]{:S(2)}) %collective-permute-start.13) | collective-permute-done | bytes 1048608 | tf_op jit(solution)/shard_map/ppermute | solution.py:32
  116.4 5.6 %collective-permute-start.16 = (f32[1,256,1024]{2,1,0:T(8,128)S(1)}, f32[1,256,1024]{2,1,0:T(8,128)S(1)}, u32[]{:S(2)}, u32[]{:S(2)}) collective-permute-start(f32[1,256,1024]{2,1,0:T(8,128)S(1)} %get-tuple-element.14), channel_id=1, source_target_pairs={{0,16},{4,20},{8,24},{12,28},{1,17},{5,21},{9,25},{13,29},{2,18},{... | collective-permute-start | bytes 3145736 | tf_op jit(solution)/shard_map/ppermute | solution.py:26
  123.4 4.5 %collective-permute-start.15 = (f32[1,1,1024]{2,1,0:T(1,128)S(1)}, f32[1,1,1024]{2,1,0:T(1,128)S(1)}, u32[]{:S(2)}, u32[]{:S(2)}) collective-permute-start(f32[1,1,1024]{2,1,0:T(1,128)S(1)} %get-tuple-element.44), channel_id=1, source_target_pairs={{0,1},{1,2},{2,3},{4,5},{5,6},{6,7},{8,9},{9,10},{10,11},{12,13},{... | collective-permute-start | bytes 12296 | tf_op jit(solution)/shard_map/ppermute | solution.py:15
  129.7 13.3 %collective-permute-done.16 = f32[1,256,1024]{2,1,0:T(8,128)S(1)} collective-permute-done((f32[1,256,1024]{2,1,0:T(8,128)S(1)}, f32[1,256,1024]{2,1,0:T(8,128)S(1)}, u32[]{:S(2)}, u32[]{:S(2)}) %collective-permute-start.16) | collective-permute-done | bytes 1048608 | tf_op jit(solution)/shard_map/ppermute | solution.py:26
  144.4 2.5 collective-permute-start.17
  146.9 20.9 %collective-permute-done.17 = f32[1,256,1024]{2,1,0:T(8,128)S(1)} collective-permute-done((f32[1,256,1024]{2,1,0:T(8,128)S(1)}, f32[1,256,1024]{2,1,0:T(8,128)S(1)}, u32[]{:S(2)}, u32[]{:S(2)}) %collective-permute-start.17) | collective-permute-done | bytes 1048608 | tf_op jit(solution)/shard_map/ppermute | solution.py:32
  170.2 4.7 %collective-permute-start.19 = (f32[1,1,1024]{2,1,0:T(1,128)S(1)}, f32[1,1,1024]{2,1,0:T(1,128)S(1)}, u32[]{:S(2)}, u32[]{:S(2)}) collective-permute-start(f32[1,1,1024]{2,1,0:T(1,128)S(1)} %get-tuple-element.42), channel_id=1, source_target_pairs={{0,1},{1,2},{2,3},{4,5},{5,6},{6,7},{8,9},{9,10},{10,11},{12,13},{... | collective-permute-start | bytes 12296 | tf_op jit(solution)/shard_map/ppermute | solution.py:15
  178.5 3.7 %collective-permute-start.23 = (f32[1,256,1024]{2,1,0:T(8,128)S(1)}, f32[1,256,1024]{2,1,0:T(8,128)S(1)}, u32[]{:S(2)}, u32[]{:S(2)}) collective-permute-start(f32[1,256,1024]{2,1,0:T(8,128)S(1)} %get-tuple-element.10), channel_id=1, source_target_pairs={{0,16},{4,20},{8,24},{12,28},{1,17},{5,21},{9,25},{13,29},{2,18},{... | collective-permute-start | bytes 3145736 | tf_op jit(solution)/shard_map/ppermute | solution.py:26
  183.5 4.8 %collective-permute-start.22 = (f32[1,1,1024]{2,1,0:T(1,128)S(1)}, f32[1,1,1024]{2,1,0:T(1,128)S(1)}, u32[]{:S(2)}, u32[]{:S(2)}) collective-permute-start(f32[1,1,1024]{2,1,0:T(1,128)S(1)} %get-tuple-element.40), channel_id=1, source_target_pairs={{0,1},{1,2},{2,3},{4,5},{5,6},{6,7},{8,9},{9,10},{10,11},{12,13},{... | collective-permute-start | bytes 12296 | tf_op jit(solution)/shard_map/ppermute | solution.py:15
  190.0 10.2 %collective-permute-done.23 = f32[1,256,1024]{2,1,0:T(8,128)S(1)} collective-permute-done((f32[1,256,1024]{2,1,0:T(8,128)S(1)}, f32[1,256,1024]{2,1,0:T(8,128)S(1)}, u32[]{:S(2)}, u32[]{:S(2)}) %collective-permute-start.23) | collective-permute-done | bytes 1048608 | tf_op jit(solution)/shard_map/ppermute | solution.py:26
  201.4 3.1 collective-permute-start.26
  205.8 4.5 %collective-permute-start.25 = (f32[1,1,1024]{2,1,0:T(1,128)S(1)}, f32[1,1,1024]{2,1,0:T(1,128)S(1)}, u32[]{:S(2)}, u32[]{:S(2)}) collective-permute-start(f32[1,1,1024]{2,1,0:T(1,128)S(1)} %get-tuple-element.38), channel_id=1, source_target_pairs={{0,1},{1,2},{2,3},{4,5},{5,6},{6,7},{8,9},{9,10},{10,11},{12,13},{... | collective-permute-start | bytes 12296 | tf_op jit(solution)/shard_map/ppermute | solution.py:15
  212.1 9.9 %collective-permute-done.26 = f32[1,256,1024]{2,1,0:T(8,128)S(1)} collective-permute-done((f32[1,256,1024]{2,1,0:T(8,128)S(1)}, f32[1,256,1024]{2,1,0:T(8,128)S(1)}, u32[]{:S(2)}, u32[]{:S(2)}) %collective-permute-start.26) | collective-permute-done | bytes 1048608 | tf_op jit(solution)/shard_map/ppermute | solution.py:26
  225.6 4.5 %collective-permute-start.28 = (f32[1,1,1024]{2,1,0:T(1,128)S(1)}, f32[1,1,1024]{2,1,0:T(1,128)S(1)}, u32[]{:S(2)}, u32[]{:S(2)}) collective-permute-start(f32[1,1,1024]{2,1,0:T(1,128)S(1)} %get-tuple-element.36), channel_id=1, source_target_pairs={{0,1},{1,2},{2,3},{4,5},{5,6},{6,7},{8,9},{9,10},{10,11},{12,13},{... | collective-permute-start | bytes 12296 | tf_op jit(solution)/shard_map/ppermute | solution.py:15
  234.7 10.2 %collective-permute-start.32 = (f32[1,256,1024]{2,1,0:T(8,128)}, f32[1,256,1024]{2,1,0:T(8,128)}, u32[]{:S(2)}, u32[]{:S(2)}) collective-permute-start(f32[1,256,1024]{2,1,0:T(8,128)} %get-tuple-element.22), channel_id=1, source_target_pairs={{0,4},{4,8},{8,12},{12,16},{16,20},{20,24},{24,28},{1,5},{5,9},{9,... | collective-permute-start | bytes 3145736 | tf_op jit(solution)/shard_map/ppermute | solution.py:26
  247.4 4.5 %collective-permute-start.31 = (f32[2,1,1024]{2,1,0:T(1,128)S(1)}, f32[2,1,1024]{2,1,0:T(1,128)S(1)}, u32[]{:S(2)}, u32[]{:S(2)}) collective-permute-start(f32[2,1,1024]{2,1,0:T(1,128)S(1)} %get-tuple-element.24), channel_id=1, source_target_pairs={{0,1},{1,2},{2,3},{4,5},{5,6},{6,7},{8,9},{9,10},{10,11},{12,13},{... | collective-permute-start | bytes 24584 | tf_op jit(solution)/shard_map/ppermute | solution.py:15
  254.8 4.8 %collective-permute-start.34 = (f32[1,1,1024]{2,1,0:T(1,128)S(1)}, f32[1,1,1024]{2,1,0:T(1,128)S(1)}, u32[]{:S(2)}, u32[]{:S(2)}) collective-permute-start(f32[1,1,1024]{2,1,0:T(1,128)S(1)} %get-tuple-element.34), channel_id=1, source_target_pairs={{0,1},{1,2},{2,3},{4,5},{5,6},{6,7},{8,9},{9,10},{10,11},{12,13},{... | collective-permute-start | bytes 12296 | tf_op jit(solution)/shard_map/ppermute | solution.py:15
  260.5 2.9 fusion.14
  265.0 3.4 %collective-permute-start.38 = (f32[1,256,1024]{2,1,0:T(8,128)}, f32[1,256,1024]{2,1,0:T(8,128)}, u32[]{:S(2)}, u32[]{:S(2)}) collective-permute-start(f32[1,256,1024]{2,1,0:T(8,128)} %get-tuple-element.18), channel_id=1, source_target_pairs={{0,4},{4,8},{8,12},{12,16},{16,20},{20,24},{24,28},{1,5},{5,9},{9,... | collective-permute-start | bytes 3145736 | tf_op jit(solution)/shard_map/ppermute | solution.py:26
  270.1 4.9 %collective-permute-start.37 = (f32[2,1,1024]{2,1,0:T(1,128)S(1)}, f32[2,1,1024]{2,1,0:T(1,128)S(1)}, u32[]{:S(2)}, u32[]{:S(2)}) collective-permute-start(f32[2,1,1024]{2,1,0:T(1,128)S(1)} %get-tuple-element.20), channel_id=1, source_target_pairs={{0,1},{1,2},{2,3},{4,5},{5,6},{6,7},{8,9},{9,10},{10,11},{12,13},{... | collective-permute-start | bytes 24584 | tf_op jit(solution)/shard_map/ppermute | solution.py:15
  279.4 3.3 %fusion.6 = f32[]{:T(128)} fusion(f32[2,256,1024]{2,1,0:T(8,128)S(1)} %copy-done.5, f32[2,258,1026]{2,1,0:T(8,128)S(1)} %select_maximum_fusion, f32[2,256,1024]{2,1,0:T(8,128)S(1)} %copy-done.2, f32[2,1,1024]{2,1,0:T(1,128)S(1)} %collective-permute-done.37, f32[2,1,1024]{2,1,0:T(1,128)S(1)} %collective-permute-done.36, f32[1,256,1024]{2,1,0:T(8,128)S(1)} %copy-done.14, ...), kind=kLoop, calls=%fused_computation.17 | loop fusion | flops 6815743 | bytes 12599300 | tf_op jit(solution)/shard_map/reduce_sum | solution.py:68
  284.7 44.9 %psum.7 = f32[6]{0:T(128)S(1)} all-reduce(f32[6]{0:T(128)S(1)} %stack.27), channel_id=1, replica_groups=mesh['tm'=8,'space'=4] {'tm','space'}, use_global_device_ids=true, to_apply=%region_6.7 | all-reduce | flops 6 | bytes 48 | tf_op jit(solution)/shard_map/psum | solution.py:112
  (125 shorter events, 67.9 us)
Async XLA Ops:
  2.5 10.9 %collective-permute-start.2 = (f32[1,256,1024]{2,1,0:T(8,128)S(1)}, f32[1,256,1024]{2,1,0:T(8,128)S(1)}, u32[]{:S(2)}, u32[]{:S(2)}) collective-permute-start(f32[1,256,1024]{2,1,0:T(8,128)S(1)} %get-tuple-element.30), channel_id=1, source_target_pairs={{0,4},{4,8},{8,12},{12,16},{16,20},{20,24},{24,28},{1,5},{5,9},{9,... | collective-permute-start | bytes 3145736 | tf_op jit(solution)/shard_map/ppermute | solution.py:26
  5.0 6.4 %collective-permute-start = (f32[2,1,1024]{2,1,0:T(1,128)S(1)}, f32[2,1,1024]{2,1,0:T(1,128)S(1)}, u32[]{:S(2)}, u32[]{:S(2)}) collective-permute-start(f32[2,1,1024]{2,1,0:T(1,128)S(1)} %get-tuple-element.33), channel_id=1, source_target_pairs={{1,0},{2,1},{3,2},{5,4},{6,5},{7,6},{9,8},{10,9},{11,10},{13,12},{... | collective-permute-start | bytes 24584 | tf_op jit(solution)/shard_map/ppermute | solution.py:18
  6.3 6.3 %collective-permute-start.1 = (f32[2,1,1024]{2,1,0:T(1,128)S(1)}, f32[2,1,1024]{2,1,0:T(1,128)S(1)}, u32[]{:S(2)}, u32[]{:S(2)}) collective-permute-start(f32[2,1,1024]{2,1,0:T(1,128)S(1)} %get-tuple-element.32), channel_id=1, source_target_pairs={{0,1},{1,2},{2,3},{4,5},{5,6},{6,7},{8,9},{9,10},{10,11},{12,13},{... | collective-permute-start | bytes 24584 | tf_op jit(solution)/shard_map/ppermute | solution.py:15
  15.5 15.8 %collective-permute-start.5 = (f32[1,256,1024]{2,1,0:T(8,128)S(1)}, f32[1,256,1024]{2,1,0:T(8,128)S(1)}, u32[]{:S(2)}, u32[]{:S(2)}) collective-permute-start(f32[1,256,1024]{2,1,0:T(8,128)S(1)} %get-tuple-element.28), channel_id=1, source_target_pairs={{0,4},{4,8},{8,12},{12,16},{16,20},{20,24},{24,28},{1,5},{5,9},{9,... | collective-permute-start | bytes 3145736 | tf_op jit(solution)/shard_map/ppermute | solution.py:26
  24.6 5.9 %collective-permute-start.4 = (f32[2,1,1024]{2,1,0:T(1,128)S(1)}, f32[2,1,1024]{2,1,0:T(1,128)S(1)}, u32[]{:S(2)}, u32[]{:S(2)}) collective-permute-start(f32[2,1,1024]{2,1,0:T(1,128)S(1)} %get-tuple-element.26), channel_id=1, source_target_pairs={{0,1},{1,2},{2,3},{4,5},{5,6},{6,7},{8,9},{9,10},{10,11},{12,13},{... | collective-permute-start | bytes 24584 | tf_op jit(solution)/shard_map/ppermute | solution.py:15
  34.0 15.7 %collective-permute-start.8 = (f32[1,256,1024]{2,1,0:T(8,128)S(1)}, f32[1,256,1024]{2,1,0:T(8,128)S(1)}, u32[]{:S(2)}, u32[]{:S(2)}) collective-permute-start(f32[1,256,1024]{2,1,0:T(8,128)S(1)} %bitcast_divide_fusion.3), channel_id=1, source_target_pairs={{0,4},{4,8},{8,12},{12,16},{16,20},{20,24},{24,28},{1,5},{5,9},{9,... | collective-permute-start | bytes 3145736 | tf_op jit(solution)/shard_map/ppermute | solution.py:26
  43.4 5.9 %collective-permute-start.7 = (f32[1,1,1024]{2,1,0:T(1,128)S(1)}, f32[1,1,1024]{2,1,0:T(1,128)S(1)}, u32[]{:S(2)}, u32[]{:S(2)}) collective-permute-start(f32[1,1,1024]{2,1,0:T(1,128)S(1)} %get-tuple-element.48), channel_id=1, source_target_pairs={{0,1},{1,2},{2,3},{4,5},{5,6},{6,7},{8,9},{9,10},{10,11},{12,13},{... | collective-permute-start | bytes 12296 | tf_op jit(solution)/shard_map/ppermute | solution.py:15
  51.2 8.8 %collective-permute-start.9 = (f32[1,256,1024]{2,1,0:T(8,128)S(1)}, f32[1,256,1024]{2,1,0:T(8,128)S(1)}, u32[]{:S(2)}, u32[]{:S(2)}) collective-permute-start(f32[1,256,1024]{2,1,0:T(8,128)S(1)} %get-tuple-element.7), channel_id=1, source_target_pairs={{0,4},{4,0},{8,12},{12,8},{16,20},{20,16},{24,28},{28,24},{1,5},{5... | collective-permute-start | bytes 3145736 | tf_op jit(solution)/shard_map/ppermute | solution.py:32
  60.4 28.1 %collective-permute-start.12 = (f32[1,256,1024]{2,1,0:T(8,128)S(1)}, f32[1,256,1024]{2,1,0:T(8,128)S(1)}, u32[]{:S(2)}, u32[]{:S(2)}) collective-permute-start(f32[1,256,1024]{2,1,0:T(8,128)S(1)} %get-tuple-element.16), channel_id=1, source_target_pairs={{0,8},{4,12},{8,16},{12,20},{16,24},{20,28},{1,9},{5,13},{9,17},{1... | collective-permute-start | bytes 3145736 | tf_op jit(solution)/shard_map/ppermute | solution.py:26
  67.0 5.9 %collective-permute-start.11 = (f32[1,1,1024]{2,1,0:T(1,128)S(1)}, f32[1,1,1024]{2,1,0:T(1,128)S(1)}, u32[]{:S(2)}, u32[]{:S(2)}) collective-permute-start(f32[1,1,1024]{2,1,0:T(1,128)S(1)} %get-tuple-element.46), channel_id=1, source_target_pairs={{0,1},{1,2},{2,3},{4,5},{5,6},{6,7},{8,9},{9,10},{10,11},{12,13},{... | collective-permute-start | bytes 12296 | tf_op jit(solution)/shard_map/ppermute | solution.py:15
  90.0 26.0 %collective-permute-start.13 = (f32[1,256,1024]{2,1,0:T(8,128)S(1)}, f32[1,256,1024]{2,1,0:T(8,128)S(1)}, u32[]{:S(2)}, u32[]{:S(2)}) collective-permute-start(f32[1,256,1024]{2,1,0:T(8,128)S(1)} %get-tuple-element.5), channel_id=1, source_target_pairs={{0,8},{4,12},{8,0},{12,4},{16,24},{20,28},{24,16},{28,20},{1,9},{5... | collective-permute-start | bytes 3145736 | tf_op jit(solution)/shard_map/ppermute | solution.py:32
  116.4 26.6 %collective-permute-start.16 = (f32[1,256,1024]{2,1,0:T(8,128)S(1)}, f32[1,256,1024]{2,1,0:T(8,128)S(1)}, u32[]{:S(2)}, u32[]{:S(2)}) collective-permute-start(f32[1,256,1024]{2,1,0:T(8,128)S(1)} %get-tuple-element.14), channel_id=1, source_target_pairs={{0,16},{4,20},{8,24},{12,28},{1,17},{5,21},{9,25},{13,29},{2,18},{... | collective-permute-start | bytes 3145736 | tf_op jit(solution)/shard_map/ppermute | solution.py:26
  123.4 5.9 %collective-permute-start.15 = (f32[1,1,1024]{2,1,0:T(1,128)S(1)}, f32[1,1,1024]{2,1,0:T(1,128)S(1)}, u32[]{:S(2)}, u32[]{:S(2)}) collective-permute-start(f32[1,1,1024]{2,1,0:T(1,128)S(1)} %get-tuple-element.44), channel_id=1, source_target_pairs={{0,1},{1,2},{2,3},{4,5},{5,6},{6,7},{8,9},{9,10},{10,11},{12,13},{... | collective-permute-start | bytes 12296 | tf_op jit(solution)/shard_map/ppermute | solution.py:15
  144.4 23.4 %collective-permute-start.17 = (f32[1,256,1024]{2,1,0:T(8,128)S(1)}, f32[1,256,1024]{2,1,0:T(8,128)S(1)}, u32[]{:S(2)}, u32[]{:S(2)}) collective-permute-start(f32[1,256,1024]{2,1,0:T(8,128)S(1)} %get-tuple-element.3), channel_id=1, source_target_pairs={{0,16},{4,20},{8,24},{12,28},{16,0},{20,4},{24,8},{28,12},{1,17},{... | collective-permute-start | bytes 3145736 | tf_op jit(solution)/shard_map/ppermute | solution.py:32
  168.2 8.3 %collective-permute-start.20 = (f32[1,256,1024]{2,1,0:T(8,128)S(1)}, f32[1,256,1024]{2,1,0:T(8,128)S(1)}, u32[]{:S(2)}, u32[]{:S(2)}) collective-permute-start(f32[1,256,1024]{2,1,0:T(8,128)S(1)} %get-tuple-element.12), channel_id=1, source_target_pairs={} | collective-permute-start | bytes 3145736 | tf_op jit(solution)/shard_map/ppermute | solution.py:26
  168.9 6.0 %collective-permute-start.18 = (f32[1,1,1024]{2,1,0:T(1,128)S(1)}, f32[1,1,1024]{2,1,0:T(1,128)S(1)}, u32[]{:S(2)}, u32[]{:S(2)}) collective-permute-start(f32[1,1,1024]{2,1,0:T(1,128)S(1)} %get-tuple-element.43), channel_id=1, source_target_pairs={{1,0},{2,1},{3,2},{5,4},{6,5},{7,6},{9,8},{10,9},{11,10},{13,12},{... | collective-permute-start | bytes 12296 | tf_op jit(solution)/shard_map/ppermute | solution.py:18
  170.2 5.9 %collective-permute-start.19 = (f32[1,1,1024]{2,1,0:T(1,128)S(1)}, f32[1,1,1024]{2,1,0:T(1,128)S(1)}, u32[]{:S(2)}, u32[]{:S(2)}) collective-permute-start(f32[1,1,1024]{2,1,0:T(1,128)S(1)} %get-tuple-element.42), channel_id=1, source_target_pairs={{0,1},{1,2},{2,3},{4,5},{5,6},{6,7},{8,9},{9,10},{10,11},{12,13},{... | collective-permute-start | bytes 12296 | tf_op jit(solution)/shard_map/ppermute | solution.py:15
  178.5 21.8 %collective-permute-start.23 = (f32[1,256,1024]{2,1,0:T(8,128)S(1)}, f32[1,256,1024]{2,1,0:T(8,128)S(1)}, u32[]{:S(2)}, u32[]{:S(2)}) collective-permute-start(f32[1,256,1024]{2,1,0:T(8,128)S(1)} %get-tuple-element.10), channel_id=1, source_target_pairs={{0,16},{4,20},{8,24},{12,28},{1,17},{5,21},{9,25},{13,29},{2,18},{... | collective-permute-start | bytes 3145736 | tf_op jit(solution)/shard_map/ppermute | solution.py:26
  182.2 6.1 %collective-permute-start.21 = (f32[1,1,1024]{2,1,0:T(1,128)S(1)}, f32[1,1,1024]{2,1,0:T(1,128)S(1)}, u32[]{:S(2)}, u32[]{:S(2)}) collective-permute-start(f32[1,1,1024]{2,1,0:T(1,128)S(1)} %get-tuple-element.41), channel_id=1, source_target_pairs={{1,0},{2,1},{3,2},{5,4},{6,5},{7,6},{9,8},{10,9},{11,10},{13,12},{... | collective-permute-start | bytes 12296 | tf_op jit(solution)/shard_map/ppermute | solution.py:18
  183.5 6.1 %collective-permute-start.22 = (f32[1,1,1024]{2,1,0:T(1,128)S(1)}, f32[1,1,1024]{2,1,0:T(1,128)S(1)}, u32[]{:S(2)}, u32[]{:S(2)}) collective-permute-start(f32[1,1,1024]{2,1,0:T(1,128)S(1)} %get-tuple-element.40), channel_id=1, source_target_pairs={{0,1},{1,2},{2,3},{4,5},{5,6},{6,7},{8,9},{9,10},{10,11},{12,13},{... | collective-permute-start | bytes 12296 | tf_op jit(solution)/shard_map/ppermute | solution.py:15
  201.4 20.6 %collective-permute-start.26 = (f32[1,256,1024]{2,1,0:T(8,128)S(1)}, f32[1,256,1024]{2,1,0:T(8,128)S(1)}, u32[]{:S(2)}, u32[]{:S(2)}) collective-permute-start(f32[1,256,1024]{2,1,0:T(8,128)S(1)} %fusion.61), channel_id=1, source_target_pairs={{0,8},{4,12},{8,16},{12,20},{16,24},{20,28},{1,9},{5,13},{9,17},{1... | collective-permute-start | bytes 3145736 | tf_op jit(solution)/shard_map/ppermute | solution.py:26
  205.8 5.9 %collective-permute-start.25 = (f32[1,1,1024]{2,1,0:T(1,128)S(1)}, f32[1,1,1024]{2,1,0:T(1,128)S(1)}, u32[]{:S(2)}, u32[]{:S(2)}) collective-permute-start(f32[1,1,1024]{2,1,0:T(1,128)S(1)} %get-tuple-element.38), channel_id=1, source_target_pairs={{0,1},{1,2},{2,3},{4,5},{5,6},{6,7},{8,9},{9,10},{10,11},{12,13},{... | collective-permute-start | bytes 12296 | tf_op jit(solution)/shard_map/ppermute | solution.py:15
  223.0 9.0 %collective-permute-start.29 = (f32[1,256,1024]{2,1,0:T(8,128)S(1)}, f32[1,256,1024]{2,1,0:T(8,128)S(1)}, u32[]{:S(2)}, u32[]{:S(2)}) collective-permute-start(f32[1,256,1024]{2,1,0:T(8,128)S(1)} %fusion.52), channel_id=1, source_target_pairs={{0,4},{4,8},{8,12},{12,16},{16,20},{20,24},{24,28},{1,5},{5,9},{9,... | collective-permute-start | bytes 3145736 | tf_op jit(solution)/shard_map/ppermute | solution.py:26
  234.7 25.8 %collective-permute-start.32 = (f32[1,256,1024]{2,1,0:T(8,128)}, f32[1,256,1024]{2,1,0:T(8,128)}, u32[]{:S(2)}, u32[]{:S(2)}) collective-permute-start(f32[1,256,1024]{2,1,0:T(8,128)} %get-tuple-element.22), channel_id=1, source_target_pairs={{0,4},{4,8},{8,12},{12,16},{16,20},{20,24},{24,28},{1,5},{5,9},{9,... | collective-permute-start | bytes 3145736 | tf_op jit(solution)/shard_map/ppermute | solution.py:26
  246.1 8.7 %collective-permute-start.30 = (f32[2,1,1024]{2,1,0:T(1,128)S(1)}, f32[2,1,1024]{2,1,0:T(1,128)S(1)}, u32[]{:S(2)}, u32[]{:S(2)}) collective-permute-start(f32[2,1,1024]{2,1,0:T(1,128)S(1)} %get-tuple-element.25), channel_id=1, source_target_pairs={{1,0},{2,1},{3,2},{5,4},{6,5},{7,6},{9,8},{10,9},{11,10},{13,12},{... | collective-permute-start | bytes 24584 | tf_op jit(solution)/shard_map/ppermute | solution.py:18
  247.4 12.2 %collective-permute-start.31 = (f32[2,1,1024]{2,1,0:T(1,128)S(1)}, f32[2,1,1024]{2,1,0:T(1,128)S(1)}, u32[]{:S(2)}, u32[]{:S(2)}) collective-permute-start(f32[2,1,1024]{2,1,0:T(1,128)S(1)} %get-tuple-element.24), channel_id=1, source_target_pairs={{0,1},{1,2},{2,3},{4,5},{5,6},{6,7},{8,9},{9,10},{10,11},{12,13},{... | collective-permute-start | bytes 24584 | tf_op jit(solution)/shard_map/ppermute | solution.py:15
  252.7 22.3 %collective-permute-start.35 = (f32[1,256,1024]{2,1,0:T(8,128)}, f32[1,256,1024]{2,1,0:T(8,128)S(1)}, u32[]{:S(2)}, u32[]{:S(2)}) collective-permute-start(f32[1,256,1024]{2,1,0:T(8,128)} %get-tuple-element.11), channel_id=1, source_target_pairs={} | collective-permute-start | bytes 3145736 | tf_op jit(solution)/shard_map/ppermute | solution.py:26
  253.5 14.9 %collective-permute-start.33 = (f32[1,1,1024]{2,1,0:T(1,128)S(1)}, f32[1,1,1024]{2,1,0:T(1,128)S(1)}, u32[]{:S(2)}, u32[]{:S(2)}) collective-permute-start(f32[1,1,1024]{2,1,0:T(1,128)S(1)} %get-tuple-element.35), channel_id=1, source_target_pairs={{1,0},{2,1},{3,2},{5,4},{6,5},{7,6},{9,8},{10,9},{11,10},{13,12},{... | collective-permute-start | bytes 12296 | tf_op jit(solution)/shard_map/ppermute | solution.py:18
  254.8 13.6 %collective-permute-start.34 = (f32[1,1,1024]{2,1,0:T(1,128)S(1)}, f32[1,1,1024]{2,1,0:T(1,128)S(1)}, u32[]{:S(2)}, u32[]{:S(2)}) collective-permute-start(f32[1,1,1024]{2,1,0:T(1,128)S(1)} %get-tuple-element.34), channel_id=1, source_target_pairs={{0,1},{1,2},{2,3},{4,5},{5,6},{6,7},{8,9},{9,10},{10,11},{12,13},{... | collective-permute-start | bytes 12296 | tf_op jit(solution)/shard_map/ppermute | solution.py:15
  265.0 13.1 %collective-permute-start.38 = (f32[1,256,1024]{2,1,0:T(8,128)}, f32[1,256,1024]{2,1,0:T(8,128)}, u32[]{:S(2)}, u32[]{:S(2)}) collective-permute-start(f32[1,256,1024]{2,1,0:T(8,128)} %get-tuple-element.18), channel_id=1, source_target_pairs={{0,4},{4,8},{8,12},{12,16},{16,20},{20,24},{24,28},{1,5},{5,9},{9,... | collective-permute-start | bytes 3145736 | tf_op jit(solution)/shard_map/ppermute | solution.py:26
  268.8 8.4 %collective-permute-start.36 = (f32[2,1,1024]{2,1,0:T(1,128)S(1)}, f32[2,1,1024]{2,1,0:T(1,128)S(1)}, u32[]{:S(2)}, u32[]{:S(2)}) collective-permute-start(f32[2,1,1024]{2,1,0:T(1,128)S(1)} %get-tuple-element.21), channel_id=1, source_target_pairs={{1,0},{2,1},{3,2},{5,4},{6,5},{7,6},{9,8},{10,9},{11,10},{13,12},{... | collective-permute-start | bytes 24584 | tf_op jit(solution)/shard_map/ppermute | solution.py:18
  270.1 7.1 %collective-permute-start.37 = (f32[2,1,1024]{2,1,0:T(1,128)S(1)}, f32[2,1,1024]{2,1,0:T(1,128)S(1)}, u32[]{:S(2)}, u32[]{:S(2)}) collective-permute-start(f32[2,1,1024]{2,1,0:T(1,128)S(1)} %get-tuple-element.20), channel_id=1, source_target_pairs={{0,1},{1,2},{2,3},{4,5},{5,6},{6,7},{8,9},{9,10},{10,11},{12,13},{... | collective-permute-start | bytes 24584 | tf_op jit(solution)/shard_map/ppermute | solution.py:15
  (22 other events, 138.5 us)
where the time goes:
time: 331 us; the launch traced here: 330 us
  starting transfers between devices  136 us (41%)
  waiting for transfers between devices  106 us (32%)
  blocking collectives  44.9 us (14%)
  other arithmetic  30.2 us (9%)
  local copies, waits for them, and re-layouts  9.38 us (3%)
  between operations  3.35 us (1%)
    ppermute x12, starting transfers between devices, with_halo(): lax.ppermute(lax.slice_in_dim(block, block.shape[dim] - width, None, axis...  56 us
    ppermute x12, starting transfers between devices, shifted(): lax.ppermute(value, axis, [(source, source + steps) for source in range(f...  52.4 us
    ppermute x12, waiting for transfers between devices, shifted(): lax.ppermute(value, axis, [(source, source + steps) for source in range(f...  48.7 us
    ppermute x3, waiting for transfers between devices, from_partner(): return lax.ppermute(value, axis, pairs)  45.8 us
    psum x1, blocking collectives, body(): totals = lax.psum(jnp.stack(partials), ('tm', 'space'))  44.9 us
    ppermute x12, starting transfers between devices, with_halo(): lax.ppermute(lax.slice_in_dim(block, 0, width, axis=dim), axis, backward)  15.5 us
    ppermute x3, starting transfers between devices, from_partner(): return lax.ppermute(value, axis, pairs)  12.4 us
    reduce_sum x6, other arithmetic, record(): local_part = jnp.sum(resid * resid) * weight_of(level)  11.6 us
  transfers between devices with their start and end apart: 39, of which 16 were waited for; matrix products, arithmetic and copies ran while one was open for 4% of the time, Pallas kernels for 0%

commit v1 on v0

--- a/solution.py
+++ b/solution.py
@@ -109,7 +109,7 @@
     diag = 1.0 + 4.0 * scaled
     resid = residual(correction, rhs, scaled, diag, 1)
     record(resid, 0)
-    totals = lax.psum(jnp.stack(partials), ("tm", "space"))
+    totals = lax.psum(lax.psum(jnp.stack(partials), "space"), "tm")
     norms = jnp.sqrt(totals / cells)
     return (correction, norms)
 

time: 331 us -> 314 us (0.949)
  blocking collectives: 44.9 us -> 26.2 us
    psum x1 -> x2, blocking collectives: 44.9 us -> 26.2 us  [body(): totals = lax.psum(lax.psum(jnp.stack(partials), 'space'), 'tm')]
where the time goes in v1:
time: 314 us; the launch traced here: 311 us
  starting transfers between devices  136 us (43%)
  waiting for transfers between devices  106 us (34%)
  other arithmetic  30.2 us (10%)
  blocking collectives  26.2 us (8%)
  local copies, waits for them, and re-layouts  9.42 us (3%)
  between operations  3.29 us (1%)
    ppermute x12, starting transfers between devices, with_halo(): lax.ppermute(lax.slice_in_dim(block, block.shape[dim] - width, None, axis...  56 us
    ppermute x12, starting transfers between devices, shifted(): lax.ppermute(value, axis, [(source, source + steps) for source in range(f...  52.4 us
    ppermute x12, waiting for transfers between devices, shifted(): lax.ppermute(value, axis, [(source, source + steps) for source in range(f...  48.7 us
    ppermute x3, waiting for transfers between devices, from_partner(): return lax.ppermute(value, axis, pairs)  45.8 us
    psum x2, blocking collectives, body(): totals = lax.psum(lax.psum(jnp.stack(partials), 'space'), 'tm')  26.2 us
    ppermute x12, starting transfers between devices, with_halo(): lax.ppermute(lax.slice_in_dim(block, 0, width, axis=dim), axis, backward)  15.5 us
    ppermute x3, starting transfers between devices, from_partner(): return lax.ppermute(value, axis, pairs)  12.4 us
    reduce_sum x6, other arithmetic, record(): local_part = jnp.sum(resid * resid) * weight_of(level)  11.6 us
  transfers between devices with their start and end apart: 39, of which 16 were waited for; matrix products, arithmetic and copies ran while one was open for 4% of the time, Pallas kernels for 0%

profile of v1, /device:TPU:0, one launch (start us, length us, event | category | flops | bytes accessed | tf_op | source)
XLA Modules:
  0.0 311.4 jit_solution(15801506467690338085)
XLA Ops:
  6.3 4.9 %collective-permute-start.1 = (f32[2,1,1024]{2,1,0:T(1,128)S(1)}, f32[2,1,1024]{2,1,0:T(1,128)S(1)}, u32[]{:S(2)}, u32[]{:S(2)}) collective-permute-start(f32[2,1,1024]{2,1,0:T(1,128)S(1)} %get-tuple-element.32), channel_id=1, source_target_pairs={{0,1},{1,2},{2,3},{4,5},{5,6},{6,7},{8,9},{9,10},{10,11},{12,13},{... | collective-permute-start | bytes 24584 | tf_op jit(solution)/shard_map/ppermute | solution.py:15
  15.5 7.8 %collective-permute-start.5 = (f32[1,256,1024]{2,1,0:T(8,128)S(1)}, f32[1,256,1024]{2,1,0:T(8,128)S(1)}, u32[]{:S(2)}, u32[]{:S(2)}) collective-permute-start(f32[1,256,1024]{2,1,0:T(8,128)S(1)} %get-tuple-element.28), channel_id=1, source_target_pairs={{0,4},{4,8},{8,12},{12,16},{16,20},{20,24},{24,28},{1,5},{5,9},{9,... | collective-permute-start | bytes 3145736 | tf_op jit(solution)/shard_map/ppermute | solution.py:26
  24.6 4.5 %collective-permute-start.4 = (f32[2,1,1024]{2,1,0:T(1,128)S(1)}, f32[2,1,1024]{2,1,0:T(1,128)S(1)}, u32[]{:S(2)}, u32[]{:S(2)}) collective-permute-start(f32[2,1,1024]{2,1,0:T(1,128)S(1)} %get-tuple-element.26), channel_id=1, source_target_pairs={{0,1},{1,2},{2,3},{4,5},{5,6},{6,7},{8,9},{9,10},{10,11},{12,13},{... | collective-permute-start | bytes 24584 | tf_op jit(solution)/shard_map/ppermute | solution.py:15
  34.0 8.1 %collective-permute-start.8 = (f32[1,256,1024]{2,1,0:T(8,128)S(1)}, f32[1,256,1024]{2,1,0:T(8,128)S(1)}, u32[]{:S(2)}, u32[]{:S(2)}) collective-permute-start(f32[1,256,1024]{2,1,0:T(8,128)S(1)} %bitcast_divide_fusion.3), channel_id=1, source_target_pairs={{0,4},{4,8},{8,12},{12,16},{16,20},{20,24},{24,28},{1,5},{5,9},{9,... | collective-permute-start | bytes 3145736 | tf_op jit(solution)/shard_map/ppermute | solution.py:26
  43.4 4.5 %collective-permute-start.7 = (f32[1,1,1024]{2,1,0:T(1,128)S(1)}, f32[1,1,1024]{2,1,0:T(1,128)S(1)}, u32[]{:S(2)}, u32[]{:S(2)}) collective-permute-start(f32[1,1,1024]{2,1,0:T(1,128)S(1)} %get-tuple-element.48), channel_id=1, source_target_pairs={{0,1},{1,2},{2,3},{4,5},{5,6},{6,7},{8,9},{9,10},{10,11},{12,13},{... | collective-permute-start | bytes 12296 | tf_op jit(solution)/shard_map/ppermute | solution.py:15
  51.2 6.5 %collective-permute-start.9 = (f32[1,256,1024]{2,1,0:T(8,128)S(1)}, f32[1,256,1024]{2,1,0:T(8,128)S(1)}, u32[]{:S(2)}, u32[]{:S(2)}) collective-permute-start(f32[1,256,1024]{2,1,0:T(8,128)S(1)} %get-tuple-element.7), channel_id=1, source_target_pairs={{0,4},{4,0},{8,12},{12,8},{16,20},{20,16},{24,28},{28,24},{1,5},{5... | collective-permute-start | bytes 3145736 | tf_op jit(solution)/shard_map/ppermute | solution.py:32
  60.4 5.3 %collective-permute-start.12 = (f32[1,256,1024]{2,1,0:T(8,128)S(1)}, f32[1,256,1024]{2,1,0:T(8,128)S(1)}, u32[]{:S(2)}, u32[]{:S(2)}) collective-permute-start(f32[1,256,1024]{2,1,0:T(8,128)S(1)} %get-tuple-element.16), channel_id=1, source_target_pairs={{0,8},{4,12},{8,16},{12,20},{16,24},{20,28},{1,9},{5,13},{9,17},{1... | collective-permute-start | bytes 3145736 | tf_op jit(solution)/shard_map/ppermute | solution.py:26
  67.0 4.5 %collective-permute-start.11 = (f32[1,1,1024]{2,1,0:T(1,128)S(1)}, f32[1,1,1024]{2,1,0:T(1,128)S(1)}, u32[]{:S(2)}, u32[]{:S(2)}) collective-permute-start(f32[1,1,1024]{2,1,0:T(1,128)S(1)} %get-tuple-element.46), channel_id=1, source_target_pairs={{0,1},{1,2},{2,3},{4,5},{5,6},{6,7},{8,9},{9,10},{10,11},{12,13},{... | collective-permute-start | bytes 12296 | tf_op jit(solution)/shard_map/ppermute | solution.py:15
  73.3 15.3 %collective-permute-done.12 = f32[1,256,1024]{2,1,0:T(8,128)S(1)} collective-permute-done((f32[1,256,1024]{2,1,0:T(8,128)S(1)}, f32[1,256,1024]{2,1,0:T(8,128)S(1)}, u32[]{:S(2)}, u32[]{:S(2)}) %collective-permute-start.12) | collective-permute-done | bytes 1048608 | tf_op jit(solution)/shard_map/ppermute | solution.py:26
  90.0 3.4 %collective-permute-start.13 = (f32[1,256,1024]{2,1,0:T(8,128)S(1)}, f32[1,256,1024]{2,1,0:T(8,128)S(1)}, u32[]{:S(2)}, u32[]{:S(2)}) collective-permute-start(f32[1,256,1024]{2,1,0:T(8,128)S(1)} %get-tuple-element.5), channel_id=1, source_target_pairs={{0,8},{4,12},{8,0},{12,4},{16,24},{20,28},{24,16},{28,20},{1,9},{5... | collective-permute-start | bytes 3145736 | tf_op jit(solution)/shard_map/ppermute | solution.py:32
  93.4 22.6 %collective-permute-done.13 = f32[1,256,1024]{2,1,0:T(8,128)S(1)} collective-permute-done((f32[1,256,1024]{2,1,0:T(8,128)S(1)}, f32[1,256,1024]{2,1,0:T(8,128)S(1)}, u32[]{:S(2)}, u32[]{:S(2)}) %collective-permute-start.13) | collective-permute-done | bytes 1048608 | tf_op jit(solution)/shard_map/ppermute | solution.py:32
  116.4 5.6 %collective-permute-start.16 = (f32[1,256,1024]{2,1,0:T(8,128)S(1)}, f32[1,256,1024]{2,1,0:T(8,128)S(1)}, u32[]{:S(2)}, u32[]{:S(2)}) collective-permute-start(f32[1,256,1024]{2,1,0:T(8,128)S(1)} %get-tuple-element.14), channel_id=1, source_target_pairs={{0,16},{4,20},{8,24},{12,28},{1,17},{5,21},{9,25},{13,29},{2,18},{... | collective-permute-start | bytes 3145736 | tf_op jit(solution)/shard_map/ppermute | solution.py:26
  123.4 4.5 %collective-permute-start.15 = (f32[1,1,1024]{2,1,0:T(1,128)S(1)}, f32[1,1,1024]{2,1,0:T(1,128)S(1)}, u32[]{:S(2)}, u32[]{:S(2)}) collective-permute-start(f32[1,1,1024]{2,1,0:T(1,128)S(1)} %get-tuple-element.44), channel_id=1, source_target_pairs={{0,1},{1,2},{2,3},{4,5},{5,6},{6,7},{8,9},{9,10},{10,11},{12,13},{... | collective-permute-start | bytes 12296 | tf_op jit(solution)/shard_map/ppermute | solution.py:15
  129.6 13.3 %collective-permute-done.16 = f32[1,256,1024]{2,1,0:T(8,128)S(1)} collective-permute-done((f32[1,256,1024]{2,1,0:T(8,128)S(1)}, f32[1,256,1024]{2,1,0:T(8,128)S(1)}, u32[]{:S(2)}, u32[]{:S(2)}) %collective-permute-start.16) | collective-permute-done | bytes 1048608 | tf_op jit(solution)/shard_map/ppermute | solution.py:26
  146.9 20.9 %collective-permute-done.17 = f32[1,256,1024]{2,1,0:T(8,128)S(1)} collective-permute-done((f32[1,256,1024]{2,1,0:T(8,128)S(1)}, f32[1,256,1024]{2,1,0:T(8,128)S(1)}, u32[]{:S(2)}, u32[]{:S(2)}) %collective-permute-start.17) | collective-permute-done | bytes 1048608 | tf_op jit(solution)/shard_map/ppermute | solution.py:32
  170.2 4.7 %collective-permute-start.19 = (f32[1,1,1024]{2,1,0:T(1,128)S(1)}, f32[1,1,1024]{2,1,0:T(1,128)S(1)}, u32[]{:S(2)}, u32[]{:S(2)}) collective-permute-start(f32[1,1,1024]{2,1,0:T(1,128)S(1)} %get-tuple-element.42), channel_id=1, source_target_pairs={{0,1},{1,2},{2,3},{4,5},{5,6},{6,7},{8,9},{9,10},{10,11},{12,13},{... | collective-permute-start | bytes 12296 | tf_op jit(solution)/shard_map/ppermute | solution.py:15
  178.4 3.7 %collective-permute-start.23 = (f32[1,256,1024]{2,1,0:T(8,128)S(1)}, f32[1,256,1024]{2,1,0:T(8,128)S(1)}, u32[]{:S(2)}, u32[]{:S(2)}) collective-permute-start(f32[1,256,1024]{2,1,0:T(8,128)S(1)} %get-tuple-element.10), channel_id=1, source_target_pairs={{0,16},{4,20},{8,24},{12,28},{1,17},{5,21},{9,25},{13,29},{2,18},{... | collective-permute-start | bytes 3145736 | tf_op jit(solution)/shard_map/ppermute | solution.py:26
  183.5 4.8 %collective-permute-start.22 = (f32[1,1,1024]{2,1,0:T(1,128)S(1)}, f32[1,1,1024]{2,1,0:T(1,128)S(1)}, u32[]{:S(2)}, u32[]{:S(2)}) collective-permute-start(f32[1,1,1024]{2,1,0:T(1,128)S(1)} %get-tuple-element.40), channel_id=1, source_target_pairs={{0,1},{1,2},{2,3},{4,5},{5,6},{6,7},{8,9},{9,10},{10,11},{12,13},{... | collective-permute-start | bytes 12296 | tf_op jit(solution)/shard_map/ppermute | solution.py:15
  190.0 10.2 %collective-permute-done.23 = f32[1,256,1024]{2,1,0:T(8,128)S(1)} collective-permute-done((f32[1,256,1024]{2,1,0:T(8,128)S(1)}, f32[1,256,1024]{2,1,0:T(8,128)S(1)}, u32[]{:S(2)}, u32[]{:S(2)}) %collective-permute-start.23) | collective-permute-done | bytes 1048608 | tf_op jit(solution)/shard_map/ppermute | solution.py:26
  201.3 3.1 collective-permute-start.26
  205.8 4.5 %collective-permute-start.25 = (f32[1,1,1024]{2,1,0:T(1,128)S(1)}, f32[1,1,1024]{2,1,0:T(1,128)S(1)}, u32[]{:S(2)}, u32[]{:S(2)}) collective-permute-start(f32[1,1,1024]{2,1,0:T(1,128)S(1)} %get-tuple-element.38), channel_id=1, source_target_pairs={{0,1},{1,2},{2,3},{4,5},{5,6},{6,7},{8,9},{9,10},{10,11},{12,13},{... | collective-permute-start | bytes 12296 | tf_op jit(solution)/shard_map/ppermute | solution.py:15
  212.0 9.9 %collective-permute-done.26 = f32[1,256,1024]{2,1,0:T(8,128)S(1)} collective-permute-done((f32[1,256,1024]{2,1,0:T(8,128)S(1)}, f32[1,256,1024]{2,1,0:T(8,128)S(1)}, u32[]{:S(2)}, u32[]{:S(2)}) %collective-permute-start.26) | collective-permute-done | bytes 1048608 | tf_op jit(solution)/shard_map/ppermute | solution.py:26
  225.6 4.5 %collective-permute-start.28 = (f32[1,1,1024]{2,1,0:T(1,128)S(1)}, f32[1,1,1024]{2,1,0:T(1,128)S(1)}, u32[]{:S(2)}, u32[]{:S(2)}) collective-permute-start(f32[1,1,1024]{2,1,0:T(1,128)S(1)} %get-tuple-element.36), channel_id=1, source_target_pairs={{0,1},{1,2},{2,3},{4,5},{5,6},{6,7},{8,9},{9,10},{10,11},{12,13},{... | collective-permute-start | bytes 12296 | tf_op jit(solution)/shard_map/ppermute | solution.py:15
  234.6 10.2 %collective-permute-start.32 = (f32[1,256,1024]{2,1,0:T(8,128)}, f32[1,256,1024]{2,1,0:T(8,128)}, u32[]{:S(2)}, u32[]{:S(2)}) collective-permute-start(f32[1,256,1024]{2,1,0:T(8,128)} %get-tuple-element.22), channel_id=1, source_target_pairs={{0,4},{4,8},{8,12},{12,16},{16,20},{20,24},{24,28},{1,5},{5,9},{9,... | collective-permute-start | bytes 3145736 | tf_op jit(solution)/shard_map/ppermute | solution.py:26
  247.3 4.5 %collective-permute-start.31 = (f32[2,1,1024]{2,1,0:T(1,128)S(1)}, f32[2,1,1024]{2,1,0:T(1,128)S(1)}, u32[]{:S(2)}, u32[]{:S(2)}) collective-permute-start(f32[2,1,1024]{2,1,0:T(1,128)S(1)} %get-tuple-element.24), channel_id=1, source_target_pairs={{0,1},{1,2},{2,3},{4,5},{5,6},{6,7},{8,9},{9,10},{10,11},{12,13},{... | collective-permute-start | bytes 24584 | tf_op jit(solution)/shard_map/ppermute | solution.py:15
  254.7 4.8 %collective-permute-start.34 = (f32[1,1,1024]{2,1,0:T(1,128)S(1)}, f32[1,1,1024]{2,1,0:T(1,128)S(1)}, u32[]{:S(2)}, u32[]{:S(2)}) collective-permute-start(f32[1,1,1024]{2,1,0:T(1,128)S(1)} %get-tuple-element.34), channel_id=1, source_target_pairs={{0,1},{1,2},{2,3},{4,5},{5,6},{6,7},{8,9},{9,10},{10,11},{12,13},{... | collective-permute-start | bytes 12296 | tf_op jit(solution)/shard_map/ppermute | solution.py:15
  260.3 2.9 fusion.14
  264.9 3.4 %collective-permute-start.38 = (f32[1,256,1024]{2,1,0:T(8,128)}, f32[1,256,1024]{2,1,0:T(8,128)}, u32[]{:S(2)}, u32[]{:S(2)}) collective-permute-start(f32[1,256,1024]{2,1,0:T(8,128)} %get-tuple-element.18), channel_id=1, source_target_pairs={{0,4},{4,8},{8,12},{12,16},{16,20},{20,24},{24,28},{1,5},{5,9},{9,... | collective-permute-start | bytes 3145736 | tf_op jit(solution)/shard_map/ppermute | solution.py:26
  270.0 4.9 %collective-permute-start.37 = (f32[2,1,1024]{2,1,0:T(1,128)S(1)}, f32[2,1,1024]{2,1,0:T(1,128)S(1)}, u32[]{:S(2)}, u32[]{:S(2)}) collective-permute-start(f32[2,1,1024]{2,1,0:T(1,128)S(1)} %get-tuple-element.20), channel_id=1, source_target_pairs={{0,1},{1,2},{2,3},{4,5},{5,6},{6,7},{8,9},{9,10},{10,11},{12,13},{... | collective-permute-start | bytes 24584 | tf_op jit(solution)/shard_map/ppermute | solution.py:15
  279.3 3.3 %fusion.6 = f32[]{:T(128)} fusion(f32[2,256,1024]{2,1,0:T(8,128)S(1)} %copy-done.5, f32[2,258,1026]{2,1,0:T(8,128)S(1)} %select_maximum_fusion, f32[2,256,1024]{2,1,0:T(8,128)S(1)} %copy-done.2, f32[2,1,1024]{2,1,0:T(1,128)S(1)} %collective-permute-done.37, f32[2,1,1024]{2,1,0:T(1,128)S(1)} %collective-permute-done.36, f32[1,256,1024]{2,1,0:T(8,128)S(1)} %copy-done.14, ...), kind=kLoop, calls=%fused_computation.17 | loop fusion | flops 6815743 | bytes 12599300 | tf_op jit(solution)/shard_map/reduce_sum | solution.py:68
  284.7 10.4 %psum.14 = f32[6]{0:T(128)S(1)} all-reduce(f32[6]{0:T(128)S(1)} %stack.27), channel_id=1, replica_groups=mesh['tm'=8,'space'=4] {'space'}, use_global_device_ids=true, to_apply=%region_6.7 | all-reduce | flops 6 | bytes 48 | tf_op jit(solution)/shard_map/psum | solution.py:112
  295.1 15.8 %psum.15 = f32[6]{0:T(128)S(1)} all-reduce(f32[6]{0:T(128)S(1)} %psum.14), channel_id=1, replica_groups=mesh['tm'=8,'space'=4] {'tm'}, use_global_device_ids=true, to_apply=%region_7.8 | all-reduce | flops 6 | bytes 48 | tf_op jit(solution)/shard_map/psum | solution.py:112
  (126 shorter events, 70.5 us)
Async XLA Ops:
  2.5 10.9 %collective-permute-start.2 = (f32[1,256,1024]{2,1,0:T(8,128)S(1)}, f32[1,256,1024]{2,1,0:T(8,128)S(1)}, u32[]{:S(2)}, u32[]{:S(2)}) collective-permute-start(f32[1,256,1024]{2,1,0:T(8,128)S(1)} %get-tuple-element.30), channel_id=1, source_target_pairs={{0,4},{4,8},{8,12},{12,16},{16,20},{20,24},{24,28},{1,5},{5,9},{9,... | collective-permute-start | bytes 3145736 | tf_op jit(solution)/shard_map/ppermute | solution.py:26
  5.0 6.4 %collective-permute-start = (f32[2,1,1024]{2,1,0:T(1,128)S(1)}, f32[2,1,1024]{2,1,0:T(1,128)S(1)}, u32[]{:S(2)}, u32[]{:S(2)}) collective-permute-start(f32[2,1,1024]{2,1,0:T(1,128)S(1)} %get-tuple-element.33), channel_id=1, source_target_pairs={{1,0},{2,1},{3,2},{5,4},{6,5},{7,6},{9,8},{10,9},{11,10},{13,12},{... | collective-permute-start | bytes 24584 | tf_op jit(solution)/shard_map/ppermute | solution.py:18
  6.3 6.3 %collective-permute-start.1 = (f32[2,1,1024]{2,1,0:T(1,128)S(1)}, f32[2,1,1024]{2,1,0:T(1,128)S(1)}, u32[]{:S(2)}, u32[]{:S(2)}) collective-permute-start(f32[2,1,1024]{2,1,0:T(1,128)S(1)} %get-tuple-element.32), channel_id=1, source_target_pairs={{0,1},{1,2},{2,3},{4,5},{5,6},{6,7},{8,9},{9,10},{10,11},{12,13},{... | collective-permute-start | bytes 24584 | tf_op jit(solution)/shard_map/ppermute | solution.py:15
  15.5 15.8 %collective-permute-start.5 = (f32[1,256,1024]{2,1,0:T(8,128)S(1)}, f32[1,256,1024]{2,1,0:T(8,128)S(1)}, u32[]{:S(2)}, u32[]{:S(2)}) collective-permute-start(f32[1,256,1024]{2,1,0:T(8,128)S(1)} %get-tuple-element.28), channel_id=1, source_target_pairs={{0,4},{4,8},{8,12},{12,16},{16,20},{20,24},{24,28},{1,5},{5,9},{9,... | collective-permute-start | bytes 3145736 | tf_op jit(solution)/shard_map/ppermute | solution.py:26
  24.6 5.9 %collective-permute-start.4 = (f32[2,1,1024]{2,1,0:T(1,128)S(1)}, f32[2,1,1024]{2,1,0:T(1,128)S(1)}, u32[]{:S(2)}, u32[]{:S(2)}) collective-permute-start(f32[2,1,1024]{2,1,0:T(1,128)S(1)} %get-tuple-element.26), channel_id=1, source_target_pairs={{0,1},{1,2},{2,3},{4,5},{5,6},{6,7},{8,9},{9,10},{10,11},{12,13},{... | collective-permute-start | bytes 24584 | tf_op jit(solution)/shard_map/ppermute | solution.py:15
  34.0 15.7 %collective-permute-start.8 = (f32[1,256,1024]{2,1,0:T(8,128)S(1)}, f32[1,256,1024]{2,1,0:T(8,128)S(1)}, u32[]{:S(2)}, u32[]{:S(2)}) collective-permute-start(f32[1,256,1024]{2,1,0:T(8,128)S(1)} %bitcast_divide_fusion.3), channel_id=1, source_target_pairs={{0,4},{4,8},{8,12},{12,16},{16,20},{20,24},{24,28},{1,5},{5,9},{9,... | collective-permute-start | bytes 3145736 | tf_op jit(solution)/shard_map/ppermute | solution.py:26
  43.4 5.9 %collective-permute-start.7 = (f32[1,1,1024]{2,1,0:T(1,128)S(1)}, f32[1,1,1024]{2,1,0:T(1,128)S(1)}, u32[]{:S(2)}, u32[]{:S(2)}) collective-permute-start(f32[1,1,1024]{2,1,0:T(1,128)S(1)} %get-tuple-element.48), channel_id=1, source_target_pairs={{0,1},{1,2},{2,3},{4,5},{5,6},{6,7},{8,9},{9,10},{10,11},{12,13},{... | collective-permute-start | bytes 12296 | tf_op jit(solution)/shard_map/ppermute | solution.py:15
  51.2 8.8 %collective-permute-start.9 = (f32[1,256,1024]{2,1,0:T(8,128)S(1)}, f32[1,256,1024]{2,1,0:T(8,128)S(1)}, u32[]{:S(2)}, u32[]{:S(2)}) collective-permute-start(f32[1,256,1024]{2,1,0:T(8,128)S(1)} %get-tuple-element.7), channel_id=1, source_target_pairs={{0,4},{4,0},{8,12},{12,8},{16,20},{20,16},{24,28},{28,24},{1,5},{5... | collective-permute-start | bytes 3145736 | tf_op jit(solution)/shard_map/ppermute | solution.py:32
  60.4 28.1 %collective-permute-start.12 = (f32[1,256,1024]{2,1,0:T(8,128)S(1)}, f32[1,256,1024]{2,1,0:T(8,128)S(1)}, u32[]{:S(2)}, u32[]{:S(2)}) collective-permute-start(f32[1,256,1024]{2,1,0:T(8,128)S(1)} %get-tuple-element.16), channel_id=1, source_target_pairs={{0,8},{4,12},{8,16},{12,20},{16,24},{20,28},{1,9},{5,13},{9,17},{1... | collective-permute-start | bytes 3145736 | tf_op jit(solution)/shard_map/ppermute | solution.py:26
  67.0 5.9 %collective-permute-start.11 = (f32[1,1,1024]{2,1,0:T(1,128)S(1)}, f32[1,1,1024]{2,1,0:T(1,128)S(1)}, u32[]{:S(2)}, u32[]{:S(2)}) collective-permute-start(f32[1,1,1024]{2,1,0:T(1,128)S(1)} %get-tuple-element.46), channel_id=1, source_target_pairs={{0,1},{1,2},{2,3},{4,5},{5,6},{6,7},{8,9},{9,10},{10,11},{12,13},{... | collective-permute-start | bytes 12296 | tf_op jit(solution)/shard_map/ppermute | solution.py:15
  90.0 26.0 %collective-permute-start.13 = (f32[1,256,1024]{2,1,0:T(8,128)S(1)}, f32[1,256,1024]{2,1,0:T(8,128)S(1)}, u32[]{:S(2)}, u32[]{:S(2)}) collective-permute-start(f32[1,256,1024]{2,1,0:T(8,128)S(1)} %get-tuple-element.5), channel_id=1, source_target_pairs={{0,8},{4,12},{8,0},{12,4},{16,24},{20,28},{24,16},{28,20},{1,9},{5... | collective-permute-start | bytes 3145736 | tf_op jit(solution)/shard_map/ppermute | solution.py:32
  116.4 26.6 %collective-permute-start.16 = (f32[1,256,1024]{2,1,0:T(8,128)S(1)}, f32[1,256,1024]{2,1,0:T(8,128)S(1)}, u32[]{:S(2)}, u32[]{:S(2)}) collective-permute-start(f32[1,256,1024]{2,1,0:T(8,128)S(1)} %get-tuple-element.14), channel_id=1, source_target_pairs={{0,16},{4,20},{8,24},{12,28},{1,17},{5,21},{9,25},{13,29},{2,18},{... | collective-permute-start | bytes 3145736 | tf_op jit(solution)/shard_map/ppermute | solution.py:26
  123.4 5.9 %collective-permute-start.15 = (f32[1,1,1024]{2,1,0:T(1,128)S(1)}, f32[1,1,1024]{2,1,0:T(1,128)S(1)}, u32[]{:S(2)}, u32[]{:S(2)}) collective-permute-start(f32[1,1,1024]{2,1,0:T(1,128)S(1)} %get-tuple-element.44), channel_id=1, source_target_pairs={{0,1},{1,2},{2,3},{4,5},{5,6},{6,7},{8,9},{9,10},{10,11},{12,13},{... | collective-permute-start | bytes 12296 | tf_op jit(solution)/shard_map/ppermute | solution.py:15
  144.4 23.4 %collective-permute-start.17 = (f32[1,256,1024]{2,1,0:T(8,128)S(1)}, f32[1,256,1024]{2,1,0:T(8,128)S(1)}, u32[]{:S(2)}, u32[]{:S(2)}) collective-permute-start(f32[1,256,1024]{2,1,0:T(8,128)S(1)} %get-tuple-element.3), channel_id=1, source_target_pairs={{0,16},{4,20},{8,24},{12,28},{16,0},{20,4},{24,8},{28,12},{1,17},{... | collective-permute-start | bytes 3145736 | tf_op jit(solution)/shard_map/ppermute | solution.py:32
  168.1 8.3 %collective-permute-start.20 = (f32[1,256,1024]{2,1,0:T(8,128)S(1)}, f32[1,256,1024]{2,1,0:T(8,128)S(1)}, u32[]{:S(2)}, u32[]{:S(2)}) collective-permute-start(f32[1,256,1024]{2,1,0:T(8,128)S(1)} %get-tuple-element.12), channel_id=1, source_target_pairs={} | collective-permute-start | bytes 3145736 | tf_op jit(solution)/shard_map/ppermute | solution.py:26
  168.9 6.0 %collective-permute-start.18 = (f32[1,1,1024]{2,1,0:T(1,128)S(1)}, f32[1,1,1024]{2,1,0:T(1,128)S(1)}, u32[]{:S(2)}, u32[]{:S(2)}) collective-permute-start(f32[1,1,1024]{2,1,0:T(1,128)S(1)} %get-tuple-element.43), channel_id=1, source_target_pairs={{1,0},{2,1},{3,2},{5,4},{6,5},{7,6},{9,8},{10,9},{11,10},{13,12},{... | collective-permute-start | bytes 12296 | tf_op jit(solution)/shard_map/ppermute | solution.py:18
  170.2 5.9 %collective-permute-start.19 = (f32[1,1,1024]{2,1,0:T(1,128)S(1)}, f32[1,1,1024]{2,1,0:T(1,128)S(1)}, u32[]{:S(2)}, u32[]{:S(2)}) collective-permute-start(f32[1,1,1024]{2,1,0:T(1,128)S(1)} %get-tuple-element.42), channel_id=1, source_target_pairs={{0,1},{1,2},{2,3},{4,5},{5,6},{6,7},{8,9},{9,10},{10,11},{12,13},{... | collective-permute-start | bytes 12296 | tf_op jit(solution)/shard_map/ppermute | solution.py:15
  178.4 21.8 %collective-permute-start.23 = (f32[1,256,1024]{2,1,0:T(8,128)S(1)}, f32[1,256,1024]{2,1,0:T(8,128)S(1)}, u32[]{:S(2)}, u32[]{:S(2)}) collective-permute-start(f32[1,256,1024]{2,1,0:T(8,128)S(1)} %get-tuple-element.10), channel_id=1, source_target_pairs={{0,16},{4,20},{8,24},{12,28},{1,17},{5,21},{9,25},{13,29},{2,18},{... | collective-permute-start | bytes 3145736 | tf_op jit(solution)/shard_map/ppermute | solution.py:26
  182.2 6.1 %collective-permute-start.21 = (f32[1,1,1024]{2,1,0:T(1,128)S(1)}, f32[1,1,1024]{2,1,0:T(1,128)S(1)}, u32[]{:S(2)}, u32[]{:S(2)}) collective-permute-start(f32[1,1,1024]{2,1,0:T(1,128)S(1)} %get-tuple-element.41), channel_id=1, source_target_pairs={{1,0},{2,1},{3,2},{5,4},{6,5},{7,6},{9,8},{10,9},{11,10},{13,12},{... | collective-permute-start | bytes 12296 | tf_op jit(solution)/shard_map/ppermute | solution.py:18
  183.5 6.1 %collective-permute-start.22 = (f32[1,1,1024]{2,1,0:T(1,128)S(1)}, f32[1,1,1024]{2,1,0:T(1,128)S(1)}, u32[]{:S(2)}, u32[]{:S(2)}) collective-permute-start(f32[1,1,1024]{2,1,0:T(1,128)S(1)} %get-tuple-element.40), channel_id=1, source_target_pairs={{0,1},{1,2},{2,3},{4,5},{5,6},{6,7},{8,9},{9,10},{10,11},{12,13},{... | collective-permute-start | bytes 12296 | tf_op jit(solution)/shard_map/ppermute | solution.py:15
  201.3 20.6 %collective-permute-start.26 = (f32[1,256,1024]{2,1,0:T(8,128)S(1)}, f32[1,256,1024]{2,1,0:T(8,128)S(1)}, u32[]{:S(2)}, u32[]{:S(2)}) collective-permute-start(f32[1,256,1024]{2,1,0:T(8,128)S(1)} %fusion.61), channel_id=1, source_target_pairs={{0,8},{4,12},{8,16},{12,20},{16,24},{20,28},{1,9},{5,13},{9,17},{1... | collective-permute-start | bytes 3145736 | tf_op jit(solution)/shard_map/ppermute | solution.py:26
  205.8 5.9 %collective-permute-start.25 = (f32[1,1,1024]{2,1,0:T(1,128)S(1)}, f32[1,1,1024]{2,1,0:T(1,128)S(1)}, u32[]{:S(2)}, u32[]{:S(2)}) collective-permute-start(f32[1,1,1024]{2,1,0:T(1,128)S(1)} %get-tuple-element.38), channel_id=1, source_target_pairs={{0,1},{1,2},{2,3},{4,5},{5,6},{6,7},{8,9},{9,10},{10,11},{12,13},{... | collective-permute-start | bytes 12296 | tf_op jit(solution)/shard_map/ppermute | solution.py:15
  222.9 9.0 %collective-permute-start.29 = (f32[1,256,1024]{2,1,0:T(8,128)S(1)}, f32[1,256,1024]{2,1,0:T(8,128)S(1)}, u32[]{:S(2)}, u32[]{:S(2)}) collective-permute-start(f32[1,256,1024]{2,1,0:T(8,128)S(1)} %fusion.52), channel_id=1, source_target_pairs={{0,4},{4,8},{8,12},{12,16},{16,20},{20,24},{24,28},{1,5},{5,9},{9,... | collective-permute-start | bytes 3145736 | tf_op jit(solution)/shard_map/ppermute | solution.py:26
  234.6 25.7 %collective-permute-start.32 = (f32[1,256,1024]{2,1,0:T(8,128)}, f32[1,256,1024]{2,1,0:T(8,128)}, u32[]{:S(2)}, u32[]{:S(2)}) collective-permute-start(f32[1,256,1024]{2,1,0:T(8,128)} %get-tuple-element.22), channel_id=1, source_target_pairs={{0,4},{4,8},{8,12},{12,16},{16,20},{20,24},{24,28},{1,5},{5,9},{9,... | collective-permute-start | bytes 3145736 | tf_op jit(solution)/shard_map/ppermute | solution.py:26
  246.0 8.7 %collective-permute-start.30 = (f32[2,1,1024]{2,1,0:T(1,128)S(1)}, f32[2,1,1024]{2,1,0:T(1,128)S(1)}, u32[]{:S(2)}, u32[]{:S(2)}) collective-permute-start(f32[2,1,1024]{2,1,0:T(1,128)S(1)} %get-tuple-element.25), channel_id=1, source_target_pairs={{1,0},{2,1},{3,2},{5,4},{6,5},{7,6},{9,8},{10,9},{11,10},{13,12},{... | collective-permute-start | bytes 24584 | tf_op jit(solution)/shard_map/ppermute | solution.py:18
  247.3 12.2 %collective-permute-start.31 = (f32[2,1,1024]{2,1,0:T(1,128)S(1)}, f32[2,1,1024]{2,1,0:T(1,128)S(1)}, u32[]{:S(2)}, u32[]{:S(2)}) collective-permute-start(f32[2,1,1024]{2,1,0:T(1,128)S(1)} %get-tuple-element.24), channel_id=1, source_target_pairs={{0,1},{1,2},{2,3},{4,5},{5,6},{6,7},{8,9},{9,10},{10,11},{12,13},{... | collective-permute-start | bytes 24584 | tf_op jit(solution)/shard_map/ppermute | solution.py:15
  252.6 22.3 %collective-permute-start.35 = (f32[1,256,1024]{2,1,0:T(8,128)}, f32[1,256,1024]{2,1,0:T(8,128)S(1)}, u32[]{:S(2)}, u32[]{:S(2)}) collective-permute-start(f32[1,256,1024]{2,1,0:T(8,128)} %get-tuple-element.11), channel_id=1, source_target_pairs={} | collective-permute-start | bytes 3145736 | tf_op jit(solution)/shard_map/ppermute | solution.py:26
  253.4 14.9 %collective-permute-start.33 = (f32[1,1,1024]{2,1,0:T(1,128)S(1)}, f32[1,1,1024]{2,1,0:T(1,128)S(1)}, u32[]{:S(2)}, u32[]{:S(2)}) collective-permute-start(f32[1,1,1024]{2,1,0:T(1,128)S(1)} %get-tuple-element.35), channel_id=1, source_target_pairs={{1,0},{2,1},{3,2},{5,4},{6,5},{7,6},{9,8},{10,9},{11,10},{13,12},{... | collective-permute-start | bytes 12296 | tf_op jit(solution)/shard_map/ppermute | solution.py:18
  254.7 13.6 %collective-permute-start.34 = (f32[1,1,1024]{2,1,0:T(1,128)S(1)}, f32[1,1,1024]{2,1,0:T(1,128)S(1)}, u32[]{:S(2)}, u32[]{:S(2)}) collective-permute-start(f32[1,1,1024]{2,1,0:T(1,128)S(1)} %get-tuple-element.34), channel_id=1, source_target_pairs={{0,1},{1,2},{2,3},{4,5},{5,6},{6,7},{8,9},{9,10},{10,11},{12,13},{... | collective-permute-start | bytes 12296 | tf_op jit(solution)/shard_map/ppermute | solution.py:15
  264.9 13.1 %collective-permute-start.38 = (f32[1,256,1024]{2,1,0:T(8,128)}, f32[1,256,1024]{2,1,0:T(8,128)}, u32[]{:S(2)}, u32[]{:S(2)}) collective-permute-start(f32[1,256,1024]{2,1,0:T(8,128)} %get-tuple-element.18), channel_id=1, source_target_pairs={{0,4},{4,8},{8,12},{12,16},{16,20},{20,24},{24,28},{1,5},{5,9},{9,... | collective-permute-start | bytes 3145736 | tf_op jit(solution)/shard_map/ppermute | solution.py:26
  268.7 8.4 %collective-permute-start.36 = (f32[2,1,1024]{2,1,0:T(1,128)S(1)}, f32[2,1,1024]{2,1,0:T(1,128)S(1)}, u32[]{:S(2)}, u32[]{:S(2)}) collective-permute-start(f32[2,1,1024]{2,1,0:T(1,128)S(1)} %get-tuple-element.21), channel_id=1, source_target_pairs={{1,0},{2,1},{3,2},{5,4},{6,5},{7,6},{9,8},{10,9},{11,10},{13,12},{... | collective-permute-start | bytes 24584 | tf_op jit(solution)/shard_map/ppermute | solution.py:18
  270.0 7.1 %collective-permute-start.37 = (f32[2,1,1024]{2,1,0:T(1,128)S(1)}, f32[2,1,1024]{2,1,0:T(1,128)S(1)}, u32[]{:S(2)}, u32[]{:S(2)}) collective-permute-start(f32[2,1,1024]{2,1,0:T(1,128)S(1)} %get-tuple-element.20), channel_id=1, source_target_pairs={{0,1},{1,2},{2,3},{4,5},{5,6},{6,7},{8,9},{9,10},{10,11},{12,13},{... | collective-permute-start | bytes 24584 | tf_op jit(solution)/shard_map/ppermute | solution.py:15
  (22 other events, 138.5 us)
